TPU v7x, 32 devices: a whole 2x2x4 slice. The times are simulated.
32 devices in a mesh: shard: 8 (over z, x), rep: 4 (over y, core).
Axes of the slice: x: 2, y: 2, z: 4, core: 2. Of those that a mesh axis runs over, the one named last changes fastest.
Arguments:
- lender_block: int32 [96, 8], P(('shard', 'rep')), may hold values from 0 to 255, as said below
- confidence: bfloat16 [96, 8, 256, 256], P(('shard', 'rep')), may hold values from 0 to 80, as said below
- lender_factors: bfloat16 [65536, 128], P('shard'), may hold values from -4 to 4
Outputs:
- borrower_factors: float32 [24576, 128], P(('shard', 'rep'))
- lender_rhs: float32 [65536, 128], P('shard')
Inputs may be any that keep to these rules, and one draw needn't show every extreme that they name: `lender_block`: within one device's 3 borrower blocks, at most 6 of the 3 x 8 entries name blocks of any one owner (block // 32), and on every device some owner is named exactly 6 times. `confidence`: about half the entries are zero; the others are positive.
All inputs are finite; a program needn't handle non-finite values.
Results may differ from a plain program's by a relative error of at most 0.0047.
Values may be sent and summed in bfloat16 or wider, within the bound.
A program may use at most 128 MiB of HBM per device.

v0:
```python
import jax
import jax.numpy as jnp
from jax import lax
from jax.sharding import PartitionSpec as P

CG_STEPS = 3
HIGH = lax.Precision.HIGHEST


def apply_system(direction, confidence, fetched, gram):
    low = direction.astype(jnp.bfloat16)
    scores = jnp.einsum("btr,bklr->bktl", low, fetched, preferred_element_type=jnp.float32)
    weighted = (confidence.astype(jnp.float32) * scores).astype(jnp.bfloat16)
    back = jnp.einsum("bktl,bklr->btr", weighted, fetched, preferred_element_type=jnp.float32)
    width = direction.shape[-1]
    global_part = jnp.dot(
        direction.reshape(-1, width), gram, precision=HIGH, preferred_element_type=jnp.float32
    )
    return global_part.reshape(direction.shape) + 0.1 * direction + back


def per_device(lender_block, confidence, lender_factors):
    shards = lax.axis_size("shard")
    blocks, lists = lender_block.shape
    tile = confidence.shape[2]
    rank = lender_factors.shape[1]
    owned = lender_factors.shape[0] // tile
    entries = blocks * lists
    slots = (2 * entries + shards - 1) // shards
    local_gram = lax.dot_general(
        lender_factors, lender_factors, (((0,), (0,)), ((), ())), preferred_element_type=jnp.float32
    )
    gram = lax.psum(local_gram, "shard")
    flat = lender_block.reshape(entries)
    owner = flat // owned
    within = flat - owner * owned
    member = (owner[:, None] == jnp.arange(shards, dtype=jnp.int32)[None, :]).astype(jnp.int32)
    position = jnp.sum(jnp.cumsum(member, axis=0) * member, axis=1) - 1
    slot_index = owner * slots + position
    requests = (
        jnp.zeros((shards * slots,), jnp.int32).at[slot_index].set(within).reshape(shards, slots)
    )
    table = lender_factors.reshape(owned, tile, rank)
    incoming = lax.all_to_all(requests, "shard", split_axis=0, concat_axis=0, tiled=True)
    replies = lax.all_to_all(table[incoming], "shard", split_axis=0, concat_axis=0, tiled=True)
    fetched = replies.reshape(shards * slots, tile, rank)[slot_index].reshape(
        blocks, lists, tile, rank
    )
    rhs = jnp.einsum("bktl,bklr->btr", confidence, fetched, preferred_element_type=jnp.float32)
    solution = jnp.zeros_like(rhs)
    resid = rhs
    direction = rhs
    norm_now = jnp.sum(resid * resid, axis=2, keepdims=True)
    for count in range(CG_STEPS):
        image = apply_system(direction, confidence, fetched, gram)
        alpha = norm_now / (jnp.sum(direction * image, axis=2, keepdims=True) + 1e-06)
        solution = solution + alpha * direction
        resid = resid - alpha * image
        norm_next = jnp.sum(resid * resid, axis=2, keepdims=True)
        direction = resid + norm_next / (norm_now + 1e-06) * direction
        norm_now = norm_next
    solved = solution.astype(jnp.bfloat16)
    partial_rhs = jnp.einsum(
        "bktl,btr->bklr", confidence, solved, preferred_element_type=jnp.float32
    )
    outgoing = (
        jnp.zeros((shards * slots, tile, rank), jnp.float32)
        .at[slot_index]
        .set(partial_rhs.reshape(entries, tile, rank))
    )
    returned = lax.all_to_all(
        outgoing.reshape(shards, slots, tile, rank),
        "shard",
        split_axis=0,
        concat_axis=0,
        tiled=True,
    )
    selector = (
        incoming.reshape(-1)[None, :] == jnp.arange(owned, dtype=jnp.int32)[:, None]
    ).astype(jnp.float32)
    owner_sum = jnp.dot(
        selector,
        returned.reshape(shards * slots, tile * rank),
        precision=HIGH,
        preferred_element_type=jnp.float32,
    )
    total = lax.psum(owner_sum, "rep")
    lenders_all = owned * tile * shards
    lender_rhs = total.reshape(owned * tile, rank) / lenders_all
    return (solution.reshape(blocks * tile, rank), lender_rhs)


def solution(mesh):
    in_specs = (P(("shard", "rep"), None), P(("shard", "rep"), None, None, None), P("shard", None))
    out_specs = (P(("shard", "rep"), None), P("shard", None))
    return jax.shard_map(
        per_device, mesh=mesh, in_specs=in_specs, out_specs=out_specs, check_vma=False
    )
```

profile of v0, /device:TPU:0, one launch (start us, length us, event | category | flops | bytes accessed | tf_op | source)
XLA Modules:
  0.0 416.2 jit_solution(9014133852448018927)
XLA Ops:
  7.2 0.0 copy-start
  7.2 0.9 reshape.224
  8.1 0.8 reshape.223
  8.9 0.1 fusion.50
  9.0 0.2 select_reduce_fusion
  9.2 0.6 scatter_custom_fusion
  9.8 0.1 all_to_all.14
  9.9 13.6 %all_to_all.22 = s32[8,1,6]{2,1,0:T(1,128)S(1)} all-to-all(s32[8,1,6]{2,1,0:T(1,128)S(1)} %bitcast.112), channel_id=1, replica_groups=mesh['shard'=8,'rep'=4] {'shard'}, dimensions={0} | all-to-all | bytes 384 | tf_op jit(solution)/shard_map/all_to_all | solution.py:44
  23.5 0.1 copy.32
  23.6 0.1 copy.33
  23.7 0.1 reshape.233
  23.8 2.7 gather_fusion
  26.5 4.4 %all-to-all-start.1 = ((bf16[8,6,256,128]{3,2,1,0:T(8,128)(2,1)}), bf16[8,6,256,128]{3,2,1,0:T(8,128)(2,1)}, u32[]{:S(2)}, u32[]{:S(2)}) async-start(bf16[8,6,256,128]{3,2,1,0:T(8,128)(2,1)} %bitcast.106), calls=%async_computation.1 | async-start | bytes 6291456 | tf_op jit(solution)/shard_map/all_to_all | solution.py:45
  30.9 0.0 all-reduce.3.cloned.1.call-start
  31.0 1.4 fusion.55
  32.4 0.0 all-reduce.3.cloned.1.call-update
  32.4 4.7 %copy.37 = bf16[3,8,256,256]{2,3,1,0:T(8,128)(2,1)} copy(bf16[3,8,256,256]{3,2,1,0:T(8,128)(2,1)} %param.4) | data formatting | bytes 6291456 | tf_op args[1]
  37.1 64.9 %all-to-all-done.1 = bf16[8,6,256,128]{3,2,1,0:T(8,128)(2,1)} async-done(((bf16[8,6,256,128]{3,2,1,0:T(8,128)(2,1)}), bf16[8,6,256,128]{3,2,1,0:T(8,128)(2,1)}, u32[]{:S(2)}, u32[]{:S(2)}) %all-to-all-start.1) | async-done | bytes 3145760 | tf_op jit(solution)/shard_map/all_to_all | solution.py:45
  102.0 3.8 gather_fusion.1
  105.8 3.5 convolution_bitcast_fusion
  109.4 4.3 %fusion.18 = f32[3,256,128]{1,2,0:T(8,128)S(1)} fusion(bf16[3,8,256,128]{3,2,1,0:T(8,128)(2,1)} %bitcast.108, bf16[3,8,256,256]{2,3,1,0:T(8,128)(2,1)} %copy.37, f32[3,256,128]{1,2,0:T(8,128)S(1)} %convolution_bitcast_fusion), kind=kOutput, calls=%fused_computation.20 | convolution fusion | flops 810123264 | bytes 5505024 | tf_op jit(solution)/shard_map/bktl,bklr->btr/dot_general | solution.py:14
  113.7 13.5 %all-reduce.3.cloned.1.call-done = f32[128,128]{1,0:T(8,128)} async-done(((f32[128,128]{1,0:T(8,128)}), f32[128,128]{1,0:T(8,128)}) %all-reduce.3.cloned.1.call-update) | async-done | bytes 65552 | tf_op jit(solution)/shard_map/psum | solution.py:33
  127.2 1.4 multiply_reduce_fusion.3
  128.6 0.1 multiply_reduce_fusion.2
  128.7 0.1 multiply_add_fusion.2
  128.8 5.1 %fusion.21 = f32[3,256,128]{1,2,0:T(8,128)} fusion(bf16[3,8,256,128]{3,2,1,0:T(8,128)(2,1)} %bitcast.109, bf16[3,8,256,256]{2,3,1,0:T(8,128)(2,1)} %copy.37, f32[3,256,128]{1,2,0:T(8,128)S(1)} %multiply_add_fusion.2), kind=kOutput, calls=%fused_computation.21 | convolution fusion | flops 810123264 | bytes 5505024 | tf_op jit(solution)/shard_map/bktl,bklr->btr/dot_general | solution.py:14
  133.8 1.6 multiply_reduce_fusion.1
  135.4 0.1 multiply_reduce_fusion
  135.5 0.8 multiply_add_fusion.1
  136.3 5.2 %fusion.24 = f32[3,256,128]{1,2,0:T(8,128)} fusion(bf16[3,8,256,128]{3,2,1,0:T(8,128)(2,1)} %bitcast.110, bf16[3,8,256,256]{2,3,1,0:T(8,128)(2,1)} %copy.37, f32[3,256,128]{1,2,0:T(8,128)} %multiply_add_fusion.1), kind=kOutput, calls=%fused_computation.22 | convolution fusion | flops 810123264 | bytes 5505024 | tf_op jit(solution)/shard_map/bktl,bklr->btr/dot_general | solution.py:14
  141.5 1.6 fusion.31
  143.1 1.1 multiply_add_fusion
  144.2 4.1 fusion.38
  148.3 3.6 copy.52
  151.9 3.4 broadcast_in_dim.5
  155.3 7.9 %scatter_fusion = f32[48,256,128]{2,1,0:T(8,128)} fusion(f32[48,256,128]{2,1,0:T(8,128)} %broadcast_in_dim.5, s32[24]{0:T(128)S(1)} %fusion.52, f32[24,256,128]{2,1,0:T(8,128)} %copy.52), kind=kCustom, calls=%fused_computation.3 | custom fusion | bytes 9437280 | tf_op jit(solution)/shard_map/scatter | solution.py:69
  163.3 4.8 %all-to-all-start.2 = ((f32[8,6,256,128]{3,2,1,0:T(8,128)}), f32[8,6,256,128]{3,2,1,0:T(8,128)}, u32[]{:S(2)}, u32[]{:S(2)}) async-start(f32[8,6,256,128]{3,2,1,0:T(8,128)} %bitcast.104), calls=%async_computation.2 | async-start | bytes 12582912 | tf_op jit(solution)/shard_map/all_to_all | solution.py:71
  168.0 0.2 all-reduce.5.cloned.1.call-start
  168.2 0.5 broadcast.206
  168.8 0.7 reduce.3
  169.4 0.1 eq.31
  169.5 135.1 %all-to-all-done.2 = f32[8,6,256,128]{3,2,1,0:T(8,128)} async-done(((f32[8,6,256,128]{3,2,1,0:T(8,128)}), f32[8,6,256,128]{3,2,1,0:T(8,128)}, u32[]{:S(2)}, u32[]{:S(2)}) %all-to-all-start.2) | async-done | bytes 6291488 | tf_op jit(solution)/shard_map/all_to_all | solution.py:71
  304.6 10.8 %fusion.3 = f32[32,32768]{1,0:T(8,128)} fusion(f32[6,8,256,128]{3,2,1,0:T(8,128)} %bitcast.40, s32[48]{0:T(128)S(1)} %eq.31), kind=kOutput, calls=%fused_computation.10 | convolution fusion | flops 603981312 | bytes 10485952 | tf_op jit(solution)/shard_map/dot_general | solution.py:81
  315.4 0.0 all-reduce.5.cloned.1.call-update
  315.4 0.9 copy.51
  316.3 83.7 %all-reduce.5.cloned.1.call-done = f32[32,32768]{1,0:T(8,128)} async-done(((f32[32,32768]{1,0:T(8,128)}), f32[32,32768]{1,0:T(8,128)}) %all-reduce.5.cloned.1.call-update) | async-done | bytes 4194320 | tf_op jit(solution)/shard_map/psum | solution.py:87
  400.0 4.4 %broadcast_multiply_fusion = f32[32,32768]{1,0:T(8,128)} fusion(f32[32,32768]{1,0:T(8,128)} %all-reduce.5.cloned.1.call-done), kind=kLoop, calls=%fused_computation.19 | loop fusion | flops 1048576 | bytes 8388608 | tf_op jit(solution)/shard_map/div | solution.py:89
  404.5 4.9 %div.83 = f32[8192,128]{1,0:T(8,128)} reshape(f32[32,32768]{1,0:T(8,128)} %broadcast_multiply_fusion) | data formatting | bytes 8388608 | tf_op jit(solution)/shard_map/div | solution.py:89
  (16 shorter events, 0.1 us)
Async XLA Ops:
  7.2 16.6 %copy-start = (bf16[8192,128]{1,0:T(8,128)(2,1)S(1)}, bf16[8192,128]{1,0:T(8,128)(2,1)}, u32[]{:S(2)}) copy-start(bf16[8192,128]{1,0:T(8,128)(2,1)} %param.5) | copy-start | bytes 6291460
  26.5 75.5 %all-to-all-start.1 = ((bf16[8,6,256,128]{3,2,1,0:T(8,128)(2,1)}), bf16[8,6,256,128]{3,2,1,0:T(8,128)(2,1)}, u32[]{:S(2)}, u32[]{:S(2)}) async-start(bf16[8,6,256,128]{3,2,1,0:T(8,128)(2,1)} %bitcast.106), calls=%async_computation.1 | async-start | bytes 6291456 | tf_op jit(solution)/shard_map/all_to_all | solution.py:45
  30.9 96.2 %all-reduce.3.cloned.1.call-start = ((), (), s32[]{:S(2)}) async-start(), calls=%async_computation.3 | async-start | bytes 131072 | tf_op jit(solution)/shard_map/psum | solution.py:33
  128.7 5.1 %copy-start.2 = (f32[128,128]{1,0:T(8,128)S(1)}, f32[128,128]{1,0:T(8,128)}, u32[]{:S(2)}) copy-start(f32[128,128]{1,0:T(8,128)} %all-reduce.3.cloned.1.call-done) | copy-start | bytes 196612
  136.3 5.2 %copy-start.1 = (f32[3,256,128]{1,2,0:T(8,128)S(1)}, f32[3,256,128]{1,2,0:T(8,128)}, u32[]{:S(2)}) copy-start(f32[3,256,128]{1,2,0:T(8,128)} %multiply_add_fusion.1) | copy-start | bytes 1179652
  163.3 141.3 %all-to-all-start.2 = ((f32[8,6,256,128]{3,2,1,0:T(8,128)}), f32[8,6,256,128]{3,2,1,0:T(8,128)}, u32[]{:S(2)}, u32[]{:S(2)}) async-start(f32[8,6,256,128]{3,2,1,0:T(8,128)} %bitcast.104), calls=%async_computation.2 | async-start | bytes 12582912 | tf_op jit(solution)/shard_map/all_to_all | solution.py:71
  168.0 232.0 %all-reduce.5.cloned.1.call-start = ((), (), s32[]{:S(2)}) async-start(), calls=%async_computation.4 | async-start | bytes 8388608 | tf_op jit(solution)/shard_map/psum | solution.py:87
Sparse Core Ops, SparseCore 0:
  35.7 91.3 all-reduce.2
  315.5 84.4 all-reduce.4
where the time goes:
time: 417 us; the launch traced here: 416 us
  waiting for transfers between devices  297 us (71%)
  matrix products  39 us (9%)
  local copies, waits for them, and re-layouts  35.2 us (8%)
  between operations  14.2 us (3%)
  blocking collectives  13.6 us (3%)
  starting transfers between devices  9.46 us (2%)
  other arithmetic  7.59 us (2%)
    all_to_all x1, waiting for transfers between devices, per_device(): lax.all_to_all(outgoing.reshape(shards, slots, tile, rank), 'shard', spli...  135 us
    psum x1, waiting for transfers between devices, per_device(): total = lax.psum(owner_sum, 'rep')  83.7 us
    all_to_all x1, waiting for transfers between devices, per_device(): lax.all_to_all(table[incoming], 'shard', split_axis=0, concat_axis=0, til...  64.9 us
    dot_general x3, matrix products, apply_system(): jnp.einsum('bktl,bklr->btr', weighted, fetched, preferred_element_type=jn...  14.5 us
    all_to_all x1, blocking collectives, per_device(): lax.all_to_all(requests, 'shard', split_axis=0, concat_axis=0, tiled=True)  13.6 us
    psum x1, waiting for transfers between devices, per_device(): gram = lax.psum(local_gram, 'shard')  13.5 us
    dot_general x1, matrix products, per_device(): jnp.dot(selector, returned.reshape(shards * slots, tile * rank), precisio...  10.8 us
  transfers between devices with their start and end apart: 4, of which 4 were waited for; matrix products, arithmetic and copies ran while one was open for 5% of the time, Pallas kernels for 0%

commit v1 on v0

--- a/solution.py
+++ b/solution.py
@@ -30,7 +30,9 @@
     local_gram = lax.dot_general(
         lender_factors, lender_factors, (((0,), (0,)), ((), ())), preferred_element_type=jnp.float32
     )
-    gram = lax.psum(local_gram, "shard")
+    gram = local_gram
+    for hop in (1, 2, 4):
+        gram = gram + lax.ppermute(gram, "shard", [(dev, dev ^ hop) for dev in range(8)])
     flat = lender_block.reshape(entries)
     owner = flat // owned
     within = flat - owner * owned

time: 417 us -> 403 us (0.966)
  waiting for transfers between devices: 297 us -> 278 us
  starting transfers between devices: 9.46 us -> 16.2 us
    all_to_all x1, waiting for transfers between devices: 64.9 us -> 16 us  [per_device(): lax.all_to_all(table[incoming], 'shard', split_axis=0, concat_axis=0, til...]
    ppermute x0 -> x3, waiting for transfers between devices: none -> 43.4 us  [per_device(): lax.ppermute(gram, 'shard', [(dev, dev ^ hop) for dev in range(8)])]
    psum x1 -> x0, waiting for transfers between devices: 13.5 us -> none  [per_device(): gram = lax.psum(local_gram, 'shard')]
    ppermute x0 -> x3, starting transfers between devices: none -> 6.77 us  [per_device(): lax.ppermute(gram, 'shard', [(dev, dev ^ hop) for dev in range(8)])]
  transfers between devices with their start and end apart: 4 -> 6, of which waited for: 4 -> 5; matrix products, arithmetic and copies ran while one was open for 5% -> 5% of each run, Pallas kernels for 0% -> 0%
where the time goes in v1:
time: 403 us
  waiting for transfers between devices  278 us (69%)
  matrix products  37.5 us (9%)
  local copies, waits for them, and re-layouts  35.2 us (9%)
  starting transfers between devices  16.2 us (4%)
  between operations  14.2 us (4%)
  blocking collectives  13.6 us (3%)
  other arithmetic  7.61 us (2%)
    all_to_all x1, waiting for transfers between devices, per_device(): lax.all_to_all(outgoing.reshape(shards, slots, tile, rank), 'shard', spli...  135 us
    psum x1, waiting for transfers between devices, per_device(): total = lax.psum(owner_sum, 'rep')  83.9 us
    ppermute x3, waiting for transfers between devices, per_device(): lax.ppermute(gram, 'shard', [(dev, dev ^ hop) for dev in range(8)])  43.4 us
    all_to_all x1, waiting for transfers between devices, per_device(): lax.all_to_all(table[incoming], 'shard', split_axis=0, concat_axis=0, til...  16 us
    dot_general x3, matrix products, apply_system(): jnp.einsum('bktl,bklr->btr', weighted, fetched, preferred_element_type=jn...  14.5 us
    all_to_all x1, blocking collectives, per_device(): lax.all_to_all(requests, 'shard', split_axis=0, concat_axis=0, tiled=True)  13.6 us
    dot_general x1, matrix products, per_device(): jnp.dot(selector, returned.reshape(shards * slots, tile * rank), precisio...  10.8 us
  transfers between devices with their start and end apart: 6, of which 5 were waited for; matrix products, arithmetic and copies ran while one was open for 5% of the time, Pallas kernels for 0%

profile of v1, /device:TPU:0, one launch (start us, length us, event | category | flops | bytes accessed | tf_op | source)
XLA Modules:
  0.0 402.7 jit_solution(14195204897366665761)
XLA Ops:
  7.2 0.9 reshape.224
  8.1 0.8 reshape.223
  8.9 0.1 fusion.50
  9.0 0.2 select_reduce_fusion
  9.2 0.6 scatter_custom_fusion
  9.8 0.1 all_to_all.14
  9.9 13.6 %all_to_all.22 = s32[8,1,6]{2,1,0:T(1,128)S(1)} all-to-all(s32[8,1,6]{2,1,0:T(1,128)S(1)} %bitcast.112), channel_id=1, replica_groups=mesh['shard'=8,'rep'=4] {'shard'}, dimensions={0} | all-to-all | bytes 384 | tf_op jit(solution)/shard_map/all_to_all | solution.py:46
  23.5 0.1 copy.32
  23.6 0.1 copy.33
  23.7 0.1 reshape.233
  23.8 2.7 gather_fusion
  26.5 4.4 %all-to-all-start.1 = ((bf16[8,6,256,128]{3,2,1,0:T(8,128)(2,1)}), bf16[8,6,256,128]{3,2,1,0:T(8,128)(2,1)}, u32[]{:S(2)}, u32[]{:S(2)}) async-start(bf16[8,6,256,128]{3,2,1,0:T(8,128)(2,1)} %bitcast.106), calls=%async_computation.1 | async-start | bytes 6291456 | tf_op jit(solution)/shard_map/all_to_all | solution.py:47
  30.9 0.8 fusion.58
  31.7 2.0 collective-permute-start
  33.6 4.7 %copy.37 = bf16[3,8,256,256]{2,3,1,0:T(8,128)(2,1)} copy(bf16[3,8,256,256]{3,2,1,0:T(8,128)(2,1)} %param.4) | data formatting | bytes 6291456 | tf_op args[1]
  38.3 19.2 %collective-permute-done = f32[128,128]{1,0:T(8,128)S(1)} collective-permute-done((f32[128,128]{1,0:T(8,128)S(1)}, f32[128,128]{1,0:T(8,128)S(1)}, u32[]{:S(2)}, u32[]{:S(2)}) %collective-permute-start) | collective-permute-done | bytes 65568 | tf_op jit(solution)/shard_map/ppermute | solution.py:35
  57.5 0.8 collective-permute-start.1
  58.3 24.2 %collective-permute-done.1 = f32[128,128]{1,0:T(8,128)S(1)} collective-permute-done((f32[128,128]{1,0:T(8,128)S(1)}, f32[128,128]{1,0:T(8,128)S(1)}, u32[]{:S(2)}, u32[]{:S(2)}) %collective-permute-start.1) | collective-permute-done | bytes 65568 | tf_op jit(solution)/shard_map/ppermute | solution.py:35
  82.6 4.0 %collective-permute-start.2 = (f32[128,128]{1,0:T(8,128)S(1)}, f32[128,128]{1,0:T(8,128)S(1)}, u32[]{:S(2)}, u32[]{:S(2)}) collective-permute-start(f32[128,128]{1,0:T(8,128)S(1)} %add.141), channel_id=1, source_target_pairs={{0,16},{4,20},{8,24},{12,28},{16,0},{20,4},{24,8},{28,12},{1,17},{... | collective-permute-start | bytes 196616 | tf_op jit(solution)/shard_map/ppermute | solution.py:35
  86.6 16.0 %all-to-all-done.1 = bf16[8,6,256,128]{3,2,1,0:T(8,128)(2,1)} async-done(((bf16[8,6,256,128]{3,2,1,0:T(8,128)(2,1)}), bf16[8,6,256,128]{3,2,1,0:T(8,128)(2,1)}, u32[]{:S(2)}, u32[]{:S(2)}) %all-to-all-start.1) | async-done | bytes 3145760 | tf_op jit(solution)/shard_map/all_to_all | solution.py:47
  102.6 3.8 gather_fusion.1
  106.4 3.5 convolution_bitcast_fusion
  110.0 4.3 %fusion.18 = f32[3,256,128]{1,2,0:T(8,128)S(1)} fusion(bf16[3,8,256,128]{3,2,1,0:T(8,128)(2,1)} %bitcast.108, bf16[3,8,256,256]{2,3,1,0:T(8,128)(2,1)} %copy.37, f32[3,256,128]{1,2,0:T(8,128)S(1)} %convolution_bitcast_fusion), kind=kOutput, calls=%fused_computation.20 | convolution fusion | flops 810123264 | bytes 5505024 | tf_op jit(solution)/shard_map/bktl,bklr->btr/dot_general | solution.py:14
  114.3 0.6 multiply_reduce_fusion.3
  114.9 0.1 multiply_reduce_fusion.2
  115.0 0.1 multiply_add_fusion.2
  115.0 5.0 %fusion.21 = f32[3,256,128]{1,2,0:T(8,128)} fusion(bf16[3,8,256,128]{3,2,1,0:T(8,128)(2,1)} %bitcast.109, bf16[3,8,256,256]{2,3,1,0:T(8,128)(2,1)} %copy.37, f32[3,256,128]{1,2,0:T(8,128)S(1)} %multiply_add_fusion.2), kind=kOutput, calls=%fused_computation.21 | convolution fusion | flops 810123264 | bytes 5505024 | tf_op jit(solution)/shard_map/bktl,bklr->btr/dot_general | solution.py:14
  120.1 1.6 multiply_reduce_fusion.1
  121.6 0.1 multiply_reduce_fusion
  121.7 0.8 multiply_add_fusion.1
  122.6 5.2 %fusion.24 = f32[3,256,128]{1,2,0:T(8,128)} fusion(bf16[3,8,256,128]{3,2,1,0:T(8,128)(2,1)} %bitcast.110, bf16[3,8,256,256]{2,3,1,0:T(8,128)(2,1)} %copy.37, f32[3,256,128]{1,2,0:T(8,128)} %multiply_add_fusion.1), kind=kOutput, calls=%fused_computation.22 | convolution fusion | flops 810123264 | bytes 5505024 | tf_op jit(solution)/shard_map/bktl,bklr->btr/dot_general | solution.py:14
  127.8 1.6 fusion.31
  129.3 1.1 multiply_add_fusion
  130.4 4.1 %fusion.38 = f32[3,128,8,256]{3,1,2,0:T(8,128)} fusion(bf16[3,8,256,256]{3,2,1,0:T(8,128)(2,1)} %param.4, f32[3,256,128]{1,2,0:T(8,128)S(1)} %multiply_add_fusion), kind=kOutput, calls=%fused_computation.45 | convolution fusion | flops 402751488 | bytes 6684672 | tf_op jit(solution)/shard_map/bktl,btr->bklr/dot_general | solution.py:65
  134.5 3.6 copy.52
  138.1 3.4 broadcast_in_dim.5
  141.5 7.9 %scatter_fusion = f32[48,256,128]{2,1,0:T(8,128)} fusion(f32[48,256,128]{2,1,0:T(8,128)} %broadcast_in_dim.5, s32[24]{0:T(128)S(1)} %fusion.52, f32[24,256,128]{2,1,0:T(8,128)} %copy.52), kind=kCustom, calls=%fused_computation.3 | custom fusion | bytes 9437280 | tf_op jit(solution)/shard_map/scatter | solution.py:71
  149.5 4.8 %all-to-all-start.2 = ((f32[8,6,256,128]{3,2,1,0:T(8,128)}), f32[8,6,256,128]{3,2,1,0:T(8,128)}, u32[]{:S(2)}, u32[]{:S(2)}) async-start(f32[8,6,256,128]{3,2,1,0:T(8,128)} %bitcast.104), calls=%async_computation.2 | async-start | bytes 12582912 | tf_op jit(solution)/shard_map/all_to_all | solution.py:73
  154.2 0.2 all-reduce.2.cloned.1.call-start
  154.5 0.5 broadcast.206
  155.0 0.7 reduce.3
  155.6 0.1 eq.31
  155.7 135.1 %all-to-all-done.2 = f32[8,6,256,128]{3,2,1,0:T(8,128)} async-done(((f32[8,6,256,128]{3,2,1,0:T(8,128)}), f32[8,6,256,128]{3,2,1,0:T(8,128)}, u32[]{:S(2)}, u32[]{:S(2)}) %all-to-all-start.2) | async-done | bytes 6291488 | tf_op jit(solution)/shard_map/all_to_all | solution.py:73
  290.8 10.8 %fusion.3 = f32[32,32768]{1,0:T(8,128)} fusion(f32[6,8,256,128]{3,2,1,0:T(8,128)} %bitcast.40, s32[48]{0:T(128)S(1)} %eq.31), kind=kOutput, calls=%fused_computation.10 | convolution fusion | flops 603981312 | bytes 10485952 | tf_op jit(solution)/shard_map/dot_general | solution.py:83
  301.6 0.9 copy.51
  302.6 83.9 %all-reduce.2.cloned.1.call-done = f32[32,32768]{1,0:T(8,128)} async-done(((f32[32,32768]{1,0:T(8,128)}), f32[32,32768]{1,0:T(8,128)}) %all-reduce.2.cloned.1.call-update) | async-done | bytes 4194320 | tf_op jit(solution)/shard_map/psum | solution.py:89
  386.5 4.4 %broadcast_multiply_fusion = f32[32,32768]{1,0:T(8,128)} fusion(f32[32,32768]{1,0:T(8,128)} %all-reduce.2.cloned.1.call-done), kind=kLoop, calls=%fused_computation.19 | loop fusion | flops 1048576 | bytes 8388608 | tf_op jit(solution)/shard_map/div | solution.py:91
  390.9 4.9 %div.83 = f32[8192,128]{1,0:T(8,128)} reshape(f32[32,32768]{1,0:T(8,128)} %broadcast_multiply_fusion) | data formatting | bytes 8388608 | tf_op jit(solution)/shard_map/div | solution.py:91
  (19 shorter events, 0.2 us)
Async XLA Ops:
  7.2 16.6 %copy-start = (bf16[8192,128]{1,0:T(8,128)(2,1)S(1)}, bf16[8192,128]{1,0:T(8,128)(2,1)}, u32[]{:S(2)}) copy-start(bf16[8192,128]{1,0:T(8,128)(2,1)} %param.5) | copy-start | bytes 6291460
  26.5 76.1 %all-to-all-start.1 = ((bf16[8,6,256,128]{3,2,1,0:T(8,128)(2,1)}), bf16[8,6,256,128]{3,2,1,0:T(8,128)(2,1)}, u32[]{:S(2)}, u32[]{:S(2)}) async-start(bf16[8,6,256,128]{3,2,1,0:T(8,128)(2,1)} %bitcast.106), calls=%async_computation.1 | async-start | bytes 6291456 | tf_op jit(solution)/shard_map/all_to_all | solution.py:47
  31.7 25.8 %collective-permute-start = (f32[128,128]{1,0:T(8,128)S(1)}, f32[128,128]{1,0:T(8,128)S(1)}, u32[]{:S(2)}, u32[]{:S(2)}) collective-permute-start(f32[128,128]{1,0:T(8,128)S(1)} %fusion.58), channel_id=1, source_target_pairs={{0,4},{4,0},{8,12},{12,8},{16,20},{20,16},{24,28},{28,24},{1,5},{5... | collective-permute-start | bytes 196616 | tf_op jit(solution)/shard_map/ppermute | solution.py:35
  57.5 25.0 %collective-permute-start.1 = (f32[128,128]{1,0:T(8,128)S(1)}, f32[128,128]{1,0:T(8,128)S(1)}, u32[]{:S(2)}, u32[]{:S(2)}) collective-permute-start(f32[128,128]{1,0:T(8,128)S(1)} %add.140), channel_id=1, source_target_pairs={{0,8},{4,12},{8,0},{12,4},{16,24},{20,28},{24,16},{28,20},{1,9},{5... | collective-permute-start | bytes 196616 | tf_op jit(solution)/shard_map/ppermute | solution.py:35
  82.6 31.7 %collective-permute-start.2 = (f32[128,128]{1,0:T(8,128)S(1)}, f32[128,128]{1,0:T(8,128)S(1)}, u32[]{:S(2)}, u32[]{:S(2)}) collective-permute-start(f32[128,128]{1,0:T(8,128)S(1)} %add.141), channel_id=1, source_target_pairs={{0,16},{4,20},{8,24},{12,28},{16,0},{20,4},{24,8},{28,12},{1,17},{... | collective-permute-start | bytes 196616 | tf_op jit(solution)/shard_map/ppermute | solution.py:35
  122.6 5.2 %copy-start.1 = (f32[3,256,128]{1,2,0:T(8,128)S(1)}, f32[3,256,128]{1,2,0:T(8,128)}, u32[]{:S(2)}) copy-start(f32[3,256,128]{1,2,0:T(8,128)} %multiply_add_fusion.1) | copy-start | bytes 1179652
  149.5 141.3 %all-to-all-start.2 = ((f32[8,6,256,128]{3,2,1,0:T(8,128)}), f32[8,6,256,128]{3,2,1,0:T(8,128)}, u32[]{:S(2)}, u32[]{:S(2)}) async-start(f32[8,6,256,128]{3,2,1,0:T(8,128)} %bitcast.104), calls=%async_computation.2 | async-start | bytes 12582912 | tf_op jit(solution)/shard_map/all_to_all | solution.py:73
  154.2 232.3 %all-reduce.2.cloned.1.call-start = ((), (), s32[]{:S(2)}) async-start(), calls=%async_computation.3 | async-start | bytes 8388608 | tf_op jit(solution)/shard_map/psum | solution.py:89
Sparse Core Ops, SparseCore 0:
  301.8 84.6 all-reduce.1
